TPU v7x, 16 devices: a 4x2x1 block of a 4x4x8 slice. The times are simulated.
16 devices in a mesh: rep: 4 (over y, z, core), dp: 4 (over x).
Axes of the slice: x: 4, y: 2, z: 1, core: 2. Of those that a mesh axis runs over, the one named last changes fastest.
The devices are a block of a 4x4x8 slice.
Arguments:
- a: bfloat16 [16, 4, 4096, 640], P(('rep', 'dp')), parts along dimension 0
- g: bfloat16 [16, 4, 4096, 2048], P(('rep', 'dp')), parts along dimension 0
Outputs:
- output: bfloat16 [16, 640, 2048], P('rep'), parts along dimension 0
There are 4 independent parts. A program takes and returns all parts, laid end to end along the dimension named above; each array names one.
All inputs are finite; a program needn't handle non-finite values.
Results may differ from a plain program's by a relative error of at most 0.012.
Values are sent between devices in bfloat16 or wider.
A program may use at most 768 MiB of HBM per device.

v0:
```python
import jax
import jax.numpy as jnp


def solution(mesh):
    groups = mesh.shape["rep"]

    def step(a, g):
        a, g = (t.reshape(groups, -1, *t.shape[1:]) for t in (a, g))
        sums = jnp.einsum("rsntd,rsntf->rndf", a, g, preferred_element_type=jnp.float32)
        return sums.astype(jnp.bfloat16).reshape(-1, *sums.shape[2:])

    return step
```

profile of v0, /device:TPU:112, one launch (start us, length us, event | category | flops | bytes accessed | tf_op | source)
XLA Modules:
  0.0 412.6 jit_solution(10275998781801297418)
XLA Ops:
  0.0 52.4 %fusion.3 = f32[1,4,640,2048]{3,2,1,0:T(8,128)} fusion(bf16[1,4,4096,2048]{3,2,1,0:T(8,128)(2,1)} %param.1, bf16[1,4,4096,640]{3,2,1,0:T(8,128)(2,1)} %param), kind=kOutput, calls=%fused_computation.4 | convolution fusion | flops 42949672960 | bytes 109051904 | tf_op jit(solution)/rsntd,rsntf->rndf/dot_general | solution.py:10
  52.4 360.1 %all-reduce.2 = bf16[1,4,640,2048]{3,2,1,0:T(8,128)(2,1)} all-reduce(f32[1,4,640,2048]{3,2,1,0:T(8,128)} %fusion.3), channel_id=1, replica_groups=[4,4]<=[16], use_global_device_ids=true, to_apply=%add.clone | all-reduce | flops 5242880 | bytes 31457280 | tf_op jit(solution)/rsntd,rsntf->rndf/dot_general | solution.py:10
where the time goes:
time: 413 us
  blocking collectives  360 us (87%)
  matrix products  52.4 us (13%)
    dot_general x1, blocking collectives, step(): jnp.einsum('rsntd,rsntf->rndf', a, g, preferred_element_type=jnp.float32)  360 us
    dot_general x1, matrix products, step(): jnp.einsum('rsntd,rsntf->rndf', a, g, preferred_element_type=jnp.float32)  52.4 us

commit v1 on v0

v1 whole, which is shorter than its diff:
```python
import jax
import jax.numpy as jnp
from jax import lax
from jax.sharding import PartitionSpec as P


def solution(mesh):
    def local(a, g):
        sums = []
        for n in range(a.shape[1]):
            term = lax.dot_general(
                a[0, n], g[0, n], (((0,), (0,)), ((), ())), preferred_element_type=jnp.float32
            )
            sums.append(lax.psum(term.astype(jnp.bfloat16), "dp"))
        return jnp.stack(sums)

    return jax.shard_map(
        local,
        mesh=mesh,
        in_specs=(P(("rep", "dp")), P(("rep", "dp"))),
        out_specs=P("rep"),
        check_vma=False,
    )
```

time: 413 us -> 281 us (0.68)
  blocking collectives: 360 us -> 0 us
  waiting for transfers between devices: 0 us -> 189 us
  matrix products: 52.4 us -> 69 us
  between operations: 0.01 us -> 13.4 us
  other arithmetic: 0 us -> 9.86 us
    dot_general x1 -> x0, blocking collectives: 360 us -> none  [step(): jnp.einsum('rsntd,rsntf->rndf', a, g, preferred_element_type=jnp.float32)]
    psum x0 -> x1, waiting for transfers between devices: none -> 189 us  [local(): sums.append(lax.psum(term.astype(jnp.bfloat16), 'dp'))]
    dot_general x1 -> x4, matrix products: 52.4 us -> 69 us  [local(): lax.dot_general(a[0, n], g[0, n], (((0,), (0,)), ((), ())), preferred_ele...]
    another operation x0 -> x1, other arithmetic: none -> 9.86 us  [local(): return jnp.stack(sums)]
  transfers between devices with their start and end apart: 0 -> 1, of which waited for: 0 -> 1; matrix products, arithmetic and copies ran while one was open for 0% -> 0% of each run, Pallas kernels for 0% -> 0%
where the time goes in v1:
time: 281 us
  waiting for transfers between devices  189 us (67%)
  matrix products  69 us (25%)
  between operations  13.4 us (5%)
  other arithmetic  9.86 us (4%)
    psum x1, waiting for transfers between devices, local(): sums.append(lax.psum(term.astype(jnp.bfloat16), 'dp'))  189 us
    dot_general x4, matrix products, local(): lax.dot_general(a[0, n], g[0, n], (((0,), (0,)), ((), ())), preferred_ele...  69 us
    another operation x1, other arithmetic, local(): return jnp.stack(sums)  9.86 us
  transfers between devices with their start and end apart: 1, of which 1 were waited for; matrix products, arithmetic and copies ran while one was open for 0% of the time, Pallas kernels for 0%

profile of v1, /device:TPU:112, one launch (start us, length us, event | category | flops | bytes accessed | tf_op | source)
XLA Modules:
  0.0 281.1 jit_solution(17934118960245292546)
XLA Ops:
  6.5 0.0 all-reduce.3.cloned.1.call-start
  6.6 17.3 %fusion.50 = bf16[1,640,2048]{2,1,0:T(8,128)(2,1)} fusion(bf16[1,4,4096,2048]{3,2,1,0:T(8,128)(2,1)} %param.3, bf16[1,4,4096,640]{3,2,1,0:T(8,128)(2,1)} %param.2), kind=kOutput, calls=%fused_computation.27 | convolution fusion | flops 10738728960 | bytes 24641536 | tf_op jit(solution)/shard_map/dot_general | solution.py:11
  23.8 17.3 %fusion.55 = bf16[1,640,2048]{2,1,0:T(8,128)(2,1)} fusion(bf16[1,4,4096,2048]{3,2,1,0:T(8,128)(2,1)} %param.3, bf16[1,4,4096,640]{3,2,1,0:T(8,128)(2,1)} %param.2), kind=kOutput, calls=%fused_computation.28 | convolution fusion | flops 10738728960 | bytes 24641536 | tf_op jit(solution)/shard_map/dot_general | solution.py:11
  41.1 17.2 %fusion.40 = bf16[1,640,2048]{2,1,0:T(8,128)(2,1)} fusion(bf16[1,4,4096,2048]{3,2,1,0:T(8,128)(2,1)} %param.3, bf16[1,4,4096,640]{3,2,1,0:T(8,128)(2,1)} %param.2), kind=kOutput, calls=%fused_computation.25 | convolution fusion | flops 10738728960 | bytes 24641536 | tf_op jit(solution)/shard_map/dot_general | solution.py:11
  58.3 17.3 %fusion.45 = bf16[1,640,2048]{2,1,0:T(8,128)(2,1)} fusion(bf16[1,4,4096,2048]{3,2,1,0:T(8,128)(2,1)} %param.3, bf16[1,4,4096,640]{3,2,1,0:T(8,128)(2,1)} %param.2), kind=kOutput, calls=%fused_computation.26 | convolution fusion | flops 10738728960 | bytes 24641536 | tf_op jit(solution)/shard_map/dot_general | solution.py:11
  75.6 0.1 all-reduce.3.cloned.1.call-update
  75.6 188.7 %all-reduce.3.cloned.1.call-done = (bf16[1,640,2048]{2,1,0:T(8,128)(2,1)}, bf16[1,640,2048]{2,1,0:T(8,128)(2,1)}, bf16[1,640,2048]{2,1,0:T(8,128)(2,1)}, bf16[1,640,2048]{2,1,0:T(8,128)(2,1)}) async-done(((bf16[1,640,2048]{2,1,0:T(8,128)(2,1)}, bf16[1,640,2048]{2,1,0:T(8,128)(2,1)}, bf16[1,640,2048]{2,1,0:T(8,128)(2,1)}, bf16[1,640,2048]{2,1,0:T(8,128)(2,1)}), (bf16[1,640,2048]{2,1,0:T(8,128)(2,1)}, ...) | async-done | bytes 10485776 | tf_op jit(solution)/shard_map/psum | solution.py:14
  264.3 9.9 %pad_maximum_fusion = bf16[4,640,2048]{2,1,0:T(8,128)(2,1)} fusion(bf16[1,640,2048]{2,1,0:T(8,128)(2,1)} %get-tuple-element.5, bf16[1,640,2048]{2,1,0:T(8,128)(2,1)} %get-tuple-element.6, bf16[1,640,2048]{2,1,0:T(8,128)(2,1)} %get-tuple-element.7, bf16[1,640,2048]{2,1,0:T(8,128)(2,1)} %get-tuple-element.8), kind=kLoop, calls=%fused_computation.12 | loop fusion | flops 15728640 | bytes 20971520 | tf_op jit(solution)/shard_map/stack | solution.py:15
Async XLA Ops:
  6.5 257.8 %all-reduce.3.cloned.1.call-start = ((), (), s32[]{:S(2)}) async-start(), calls=%async_computation | async-start | bytes 20971520 | tf_op jit(solution)/shard_map/psum | solution.py:14
Sparse Core Ops, SparseCore 0:
  75.7 188.5 all-reduce.2

commit v2 on v1

v2 whole, which is shorter than its diff:
```python
import functools

import jax
import jax.numpy as jnp
from jax import lax
from jax.experimental import pallas as pl
from jax.experimental.pallas import tpu as pltpu
from jax.sharding import PartitionSpec as P

MESH = pl.DeviceIdType.MESH
RIGHT, LEFT = 0, 1
FAR, RAW, SUM, FIRST, SECOND, ON = range(6)
G_SLOTS = 3


def kernel(n, a, g, out, abuf, gbuf, term, snd, rcv, fin, a_sem, g_sem, send_sem, recv_sem, out_sem):
    matrices, tokens, rows = a.shape[1:]
    half = g.shape[3] // n // 2
    units = matrices * n
    me = lax.axis_index("dp")
    to = [lax.rem(me + 1, n), lax.rem(me + n - 1, n)]

    def columns(owner, h):
        return pl.ds(pl.multiple_of(owner * (2 * half) + h * half, half), half)

    def load_a(m):
        return pltpu.make_async_copy(a.at[0, m], abuf.at[lax.rem(m, 2)], a_sem.at[lax.rem(m, 2)])

    def load_g(u):
        m, k = u // n, lax.rem(u, n)
        offset = jnp.where(k == 0, 2, jnp.where(k == 1, 1, jnp.where(k == 2, n - 1, 0)))
        owner = lax.rem(me + offset, n)
        slot = lax.rem(u, G_SLOTS)
        src = g.at[0, m, :, pl.ds(pl.multiple_of(owner * (2 * half), 2 * half), 2 * half)]
        return pltpu.make_async_copy(src, gbuf.at[slot], g_sem.at[slot])

    def copy(m, kind, way):
        if kind <= SUM:
            src, dst = snd.at[m, kind, way], rcv.at[m, kind, way]
        elif kind == ON:
            where = out.at[m, :, columns(to[1 - way], way)]
            src, dst = where, where
        else:
            h = way if kind == FIRST else 1 - way
            src, dst = fin.at[m, h], out.at[m, :, columns(me, h)]
        return pltpu.make_async_remote_copy(
            src_ref=src,
            dst_ref=dst,
            send_sem=send_sem.at[m, kind, way],
            recv_sem=recv_sem.at[m, kind, way],
            device_id={"dp": to[way]},
            device_id_type=MESH,
        )

    def keep(m, h):
        return pltpu.make_async_copy(fin.at[m, h], out.at[m, :, columns(me, h)], out_sem.at[m, h])

    def send(m, kind, way, value):
        snd[m, kind, way] = value.astype(snd.dtype)
        copy(m, kind, way).start()

    def add_far(m):
        for way in (RIGHT, LEFT):
            copy(m, FAR, way).wait_recv()
            own = term[lax.rem(m, 2), 1 + way, 1 - way]
            send(m, SUM, way, own + rcv[m, FAR, way].astype(jnp.float32))

    def finish(m):
        for h in (0, 1):
            copy(m, RAW, h).wait_recv()
            copy(m, SUM, 1 - h).wait_recv()
            total = term[lax.rem(m, 2), 3, h] + rcv[m, RAW, h].astype(jnp.float32)
            total = total + rcv[m, SUM, 1 - h].astype(jnp.float32)
            fin[m, h] = total.astype(fin.dtype)
        copy(m, FIRST, RIGHT).start()
        copy(m, FIRST, LEFT).start()
        copy(m, SECOND, RIGHT).start()
        copy(m, SECOND, LEFT).start()
        for h in (0, 1):
            keep(m, h).start()

    def pass_on(m):
        for way in (RIGHT, LEFT):
            copy(m, FIRST, way).wait_recv()
            copy(m, ON, way).start()

    load_a(0).start()
    load_g(0).start()
    load_g(1).start()

    barrier = pltpu.get_barrier_semaphore()
    for way in (RIGHT, LEFT):
        pl.semaphore_signal(barrier, inc=1, device_id={"dp": to[way]}, device_id_type=MESH)
    pl.semaphore_wait(barrier, 2)

    @pl.loop(0, units)
    def unit(u):
        m, k = u // n, lax.rem(u, n)

        @pl.when(u + 2 < units)
        def _():
            load_g(u + 2).start()

        @pl.when(k == 0)
        def _():
            load_a(m).wait()

            @pl.when(m + 1 < matrices)
            def _():
                load_a(m + 1).start()

        load_g(u).wait()
        slot, side = lax.rem(u, G_SLOTS), lax.rem(m, 2)

        @pl.loop(0, 2)
        def _(h):
            at = pl.ds(pl.multiple_of(h * half, half), half)
            term[side, k, h] = lax.dot_general(
                abuf[side], gbuf[slot, :, at], (((0,), (0,)), ((), ())), preferred_element_type=jnp.float32
            )

        @pl.when(k == 0)
        def _():
            send(m, FAR, RIGHT, term[side, 0, 1])
            send(m, FAR, LEFT, term[side, 0, 0])

        @pl.when(k == 1)
        def _():
            send(m, RAW, RIGHT, term[side, 1, 0])

        @pl.when(k == 2)
        def _():
            send(m, RAW, LEFT, term[side, 2, 1])

        @pl.when(k == 3)
        def _():
            add_far(m)

            @pl.when(m >= 1)
            def _():
                finish(m - 1)

            @pl.when(m >= 2)
            def _():
                pass_on(m - 2)

    finish(matrices - 1)
    pass_on(matrices - 2)
    pass_on(matrices - 1)

    @pl.loop(0, matrices)
    def _(m):
        for h in (0, 1):
            keep(m, h).wait()
        for way in (RIGHT, LEFT):
            for kind in (SECOND, ON):
                copy(m, kind, way).wait_recv()
            for kind in range(6):
                copy(m, kind, way).wait_send()


def solution(mesh):
    n = mesh.shape["dp"]

    def local(a, g):
        matrices, tokens, rows = a.shape[1:]
        wide = g.shape[3]
        half = wide // n // 2
        bf16, f32 = jnp.bfloat16, jnp.float32
        return pl.pallas_call(
            functools.partial(kernel, n),
            out_shape=jax.ShapeDtypeStruct((matrices, rows, wide), bf16),
            in_specs=[pl.BlockSpec(memory_space=pl.ANY)] * 2,
            out_specs=pl.BlockSpec(memory_space=pl.ANY),
            scratch_shapes=[
                pltpu.VMEM((2, tokens, rows), bf16),
                pltpu.VMEM((G_SLOTS, tokens, 2 * half), bf16),
                pltpu.VMEM((2, n, 2, rows, half), f32),
                pltpu.VMEM((matrices, 3, 2, rows, half), bf16),
                pltpu.VMEM((matrices, 3, 2, rows, half), bf16),
                pltpu.VMEM((matrices, 2, rows, half), bf16),
                pltpu.SemaphoreType.DMA((2,)),
                pltpu.SemaphoreType.DMA((G_SLOTS,)),
                pltpu.SemaphoreType.DMA((matrices, 6, 2)),
                pltpu.SemaphoreType.DMA((matrices, 6, 2)),
                pltpu.SemaphoreType.DMA((matrices, 2)),
            ],
            compiler_params=pltpu.CompilerParams(
                collective_id=0, has_side_effects=True, vmem_limit_bytes=67043328
            ),
        )(a, g)

    return jax.shard_map(
        local,
        mesh=mesh,
        in_specs=(P(("rep", "dp")), P(("rep", "dp"))),
        out_specs=P("rep"),
        check_vma=False,
    )
```

time: 281 us -> 192 us (0.68)
  waiting for transfers between devices: 189 us -> 0 us
  Pallas kernels: 0 us -> 181 us
  matrix products: 69 us -> 0 us
  between operations: 13.4 us -> 0.01 us
  local copies, waits for them, and re-layouts: 0 us -> 10.3 us
  other arithmetic: 9.86 us -> 0 us
    psum x1 -> x0, waiting for transfers between devices: 189 us -> none  [local(): sums.append(lax.psum(term.astype(jnp.bfloat16), 'dp'))]
    pallas_call x0 -> x1, Pallas kernels: none -> 181 us  [local(): pl.pallas_call(functools.partial(kernel, n), out_shape=jax.ShapeDtypeStru...]
    dot_general x4 -> x0, matrix products: 69 us -> none  [local(): lax.dot_general(a[0, n], g[0, n], (((0,), (0,)), ((), ())), preferred_ele...]
    unnamed x0 -> x1, local copies, waits for them, and re-layouts: none -> 10.3 us
    another operation x1 -> x0, other arithmetic: 9.86 us -> none  [local(): return jnp.stack(sums)]
  transfers between devices with their start and end apart: 1 -> 0, of which waited for: 1 -> 0; matrix products, arithmetic and copies ran while one was open for 0% -> 0% of each run, Pallas kernels for 0% -> 0%
where the time goes in v2:
time: 192 us; the launch traced here: 191 us
  Pallas kernels  181 us (94%)
  local copies, waits for them, and re-layouts  10.3 us (5%)
    pallas_call x1, Pallas kernels, local(): pl.pallas_call(functools.partial(kernel, n), out_shape=jax.ShapeDtypeStru...  181 us
    unnamed x1, local copies, waits for them, and re-layouts  10.3 us

profile of v2, /device:TPU:112, one launch (start us, length us, event | category | flops | bytes accessed | tf_op | source)
XLA Modules:
  0.0 191.4 jit_solution(15772165979818617644)
XLA Ops:
  0.0 181.1 %shard_map.28 = bf16[4,640,2048]{2,1,0:T(8,128)(2,1)} custom-call(bf16[1,4,4096,640]{3,2,1,0:T(8,128)(2,1)} %a.1, bf16[1,4,4096,2048]{3,2,1,0:T(8,128)(2,1)} %g.1), custom_call_target="tpu_custom_call" | custom-call | tf_op jit(solution)/shard_map/pallas_call | solution.py:170
  181.1 10.3 %copy.4 = bf16[4,640,2048]{2,1,0:T(8,128)(2,1)} copy(bf16[4,640,2048]{2,1,0:T(8,128)(2,1)} %shard_map.28) | data formatting | bytes 20971520

commit v3 on v2

v3 whole, which is shorter than its diff:
```python
import functools

import jax
import jax.numpy as jnp
from jax import lax
from jax.experimental import pallas as pl
from jax.experimental.pallas import tpu as pltpu
from jax.sharding import PartitionSpec as P

MESH = pl.DeviceIdType.MESH
RIGHT, LEFT = 0, 1
FAR0, FAR1, RAW, SUM, FIRST, SECOND, ON = range(7)
KINDS = 7
G_SLOTS = 4
CUT = 256
VMEM_LIMIT = 53000000


def kernel(n, a, g, out, abuf, gbuf, term, snd, rcv, a_sem, g_sem, send_sem, recv_sem):
    matrices, tokens, rows = a.shape[1:]
    half = g.shape[3] // n // 2
    per = 2 * n
    units = matrices * per
    f32 = jnp.float32
    me = lax.axis_index("dp")
    to = [lax.rem(me + 1, n), lax.rem(me + n - 1, n)]

    def columns(owner, h):
        return pl.ds(pl.multiple_of(owner * (2 * half) + h * half, half), half)

    def load_a(m):
        return pltpu.make_async_copy(a.at[0, m], abuf.at[lax.rem(m, 2)], a_sem.at[lax.rem(m, 2)])

    def load_a_part(part):
        at = pl.ds(0, CUT) if part == 0 else pl.ds(CUT, rows - CUT)
        return pltpu.make_async_copy(a.at[0, 0, :, at], abuf.at[0, :, at], a_sem.at[2 * part])

    def pick(j, values):
        out = values[-1]
        for i, value in reversed(list(enumerate(values[:-1]))):
            out = jnp.where(j == i, value, out)
        return out

    order = [(2, 1), (2, 0), (1, 0), (n - 1, 1), (1, 1), (n - 1, 0), (0, 0), (0, 1)]

    def load_g(u):
        m, j = u // per, lax.rem(u, per)
        owner = lax.rem(me + pick(j, [o for o, _ in order]), n)
        slot = lax.rem(u, G_SLOTS)
        src = g.at[0, m, :, columns(owner, pick(j, [h for _, h in order]))]
        return pltpu.make_async_copy(src, gbuf.at[slot], g_sem.at[slot])

    def copy(m, kind, way):
        if kind in (FAR0, FAR1):
            at = pl.ds(0, CUT) if kind == FAR0 else pl.ds(CUT, rows - CUT)
            src, dst = snd.at[m, 0, way, at], rcv.at[m, 0, way, at]
        elif kind in (RAW, SUM):
            src, dst = snd.at[m, kind - 1, way], rcv.at[m, kind - 1, way]
        else:
            owner = to[1 - way] if kind == ON else me
            h = 1 - way if kind == SECOND else way
            src = dst = out.at[m, :, columns(owner, h)]
        return pltpu.make_async_remote_copy(
            src_ref=src,
            dst_ref=dst,
            send_sem=send_sem.at[m, kind, way],
            recv_sem=recv_sem.at[m, kind, way],
            device_id={"dp": to[way]},
            device_id_type=MESH,
        )

    def add_far(m):
        for way in (RIGHT, LEFT):
            copy(m, FAR0, way).wait_recv()
            copy(m, FAR1, way).wait_recv()
            total = term[1 + way] + rcv[m, 0, way].astype(f32)
            snd[m, 2, way] = total.astype(snd.dtype)
            copy(m, SUM, way).start()

    def finish(m):
        for h in (0, 1):
            copy(m, RAW, h).wait_recv()
            copy(m, SUM, 1 - h).wait_recv()
            total = term[3 + 2 * lax.rem(m, 2) + h] + rcv[m, 1, h].astype(f32)
            total = total + rcv[m, 2, 1 - h].astype(f32)
            out[m, :, columns(me, h)] = total.astype(out.dtype)
            copy(m, FIRST, h).start()
        copy(m, SECOND, RIGHT).start()
        copy(m, SECOND, LEFT).start()

    def pass_on(m):
        for way in (RIGHT, LEFT):
            copy(m, FIRST, way).wait_recv()
            copy(m, ON, way).start()

    def dot(x, y):
        return lax.dot_general(x, y, (((0,), (0,)), ((), ())), preferred_element_type=f32)

    load_g(0).start()
    load_a_part(0).start()
    load_g(1).start()
    load_a_part(1).start()
    load_g(2).start()

    barrier = pltpu.get_barrier_semaphore()
    for way in (RIGHT, LEFT):
        pl.semaphore_signal(barrier, inc=1, device_id={"dp": to[way]}, device_id_type=MESH)

    for part, kind in ((0, FAR0), (1, FAR1)):
        at = pl.ds(0, CUT) if part == 0 else pl.ds(CUT, rows - CUT)
        load_a_part(part).wait()
        for way in (RIGHT, LEFT):
            if part == 0:
                load_g(way).wait()
            snd[0, 0, way, at] = dot(abuf[0, :, at], gbuf[way]).astype(snd.dtype)
            if part == 0 and way == RIGHT:
                pl.semaphore_wait(barrier, 2)
            copy(0, kind, way).start()
    for u in (3, 4, 5):
        load_g(u).start()
    load_a(1).start()

    @pl.loop(2, units)
    def unit(u):
        m, j = u // per, lax.rem(u, per)

        @pl.when((u > 2) & (u + 3 < units))
        def _():
            load_g(u + 3).start()

        @pl.when(j == 0)
        def _():
            load_a(m).wait()

            @pl.when(m + 1 < matrices)
            def _():
                load_a(m + 1).start()

        load_g(u).wait()
        side = lax.rem(m, 2)
        slot = pick(j, [0, 0, 0, 0, 1, 2, 3 + 2 * side, 4 + 2 * side])
        term[slot] = dot(abuf[side], gbuf[lax.rem(u, G_SLOTS)])

        for way in (RIGHT, LEFT):

            @pl.when(j == way)
            def _():
                snd[m, 0, way] = term[0].astype(snd.dtype)
                copy(m, FAR0, way).start()
                copy(m, FAR1, way).start()

            @pl.when(j == 2 + way)
            def _():
                snd[m, 1, way] = term[0].astype(snd.dtype)
                copy(m, RAW, way).start()

        @pl.when(j == per - 1)
        def _():
            add_far(m)

            @pl.when(m >= 1)
            def _():
                finish(m - 1)

            @pl.when(m >= 2)
            def _():
                pass_on(m - 2)

    finish(matrices - 1)
    pass_on(matrices - 2)
    pass_on(matrices - 1)

    @pl.loop(0, matrices)
    def _(m):
        for way in (RIGHT, LEFT):
            for kind in (SECOND, ON):
                copy(m, kind, way).wait_recv()
            for kind in range(KINDS):
                copy(m, kind, way).wait_send()


def write(held, out, sem):
    pieces = []
    for m in range(held.shape[0]):
        for r in range(0, held.shape[1], held.shape[1] // 2):
            at = (m, pl.ds(r, held.shape[1] // 2))
            pieces.append(pltpu.make_async_copy(held.at[at], out.at[at], sem.at[len(pieces)]))
    for piece in pieces:
        piece.start()
    for piece in pieces:
        piece.wait()


def solution(mesh):
    n = mesh.shape["dp"]

    def local(a, g):
        matrices, tokens, rows = a.shape[1:]
        wide = g.shape[3]
        half = wide // n // 2
        bf16, f32 = jnp.bfloat16, jnp.float32
        held = pl.pallas_call(
            functools.partial(kernel, n),
            out_shape=pltpu.VMEM((matrices, rows, wide), bf16),
            in_specs=[pl.BlockSpec(memory_space=pl.ANY)] * 2,
            out_specs=pl.BlockSpec(memory_space=pltpu.VMEM),
            scratch_shapes=[
                pltpu.VMEM((2, tokens, rows), bf16),
                pltpu.VMEM((G_SLOTS, tokens, half), bf16),
                pltpu.VMEM((7, rows, half), f32),
                pltpu.VMEM((matrices, 3, 2, rows, half), bf16),
                pltpu.VMEM((matrices, 3, 2, rows, half), bf16),
                pltpu.SemaphoreType.DMA((3,)),
                pltpu.SemaphoreType.DMA((G_SLOTS,)),
                pltpu.SemaphoreType.DMA((matrices, KINDS, 2)),
                pltpu.SemaphoreType.DMA((matrices, KINDS, 2)),
            ],
            compiler_params=pltpu.CompilerParams(
                collective_id=0, has_side_effects=True, vmem_limit_bytes=VMEM_LIMIT
            ),
        )(a, g)
        return pl.pallas_call(
            write,
            out_shape=jax.ShapeDtypeStruct(held.shape, bf16),
            in_specs=[pl.BlockSpec(memory_space=pltpu.VMEM)],
            out_specs=pl.BlockSpec(memory_space=pl.ANY),
            scratch_shapes=[pltpu.SemaphoreType.DMA((2 * matrices,))],
            compiler_params=pltpu.CompilerParams(vmem_limit_bytes=2 * 1024 * 1024),
        )(pltpu.with_memory_space_constraint(held, pltpu.VMEM))

    return jax.shard_map(
        local,
        mesh=mesh,
        in_specs=(P(("rep", "dp")), P(("rep", "dp"))),
        out_specs=P("rep"),
        check_vma=False,
    )
```

time: 192 us -> 183 us (0.953)
  local copies, waits for them, and re-layouts: 10.3 us -> 0 us
  Pallas kernels: 181 us -> 183 us
    unnamed x1 -> x0, local copies, waits for them, and re-layouts: 10.3 us -> none
    pallas_call x1 -> x2, Pallas kernels: 181 us -> 183 us  [the longest x1 178 us: local(): pl.pallas_call(functools.partial(kernel, n), out_shape=pltpu.VMEM((matric...]
where the time goes in v3:
time: 183 us
  Pallas kernels  183 us (100%)
    pallas_call x1, Pallas kernels, local(): pl.pallas_call(functools.partial(kernel, n), out_shape=pltpu.VMEM((matric...  178 us
    pallas_call x1, Pallas kernels, local(): pl.pallas_call(write, out_shape=jax.ShapeDtypeStruct(held.shape, bf16), i...  4.04 us

profile of v3, /device:TPU:112, one launch (start us, length us, event | category | flops | bytes accessed | tf_op | source)
XLA Modules:
  0.0 182.5 jit_solution(10383832310695494519)
XLA Ops:
  0.0 178.5 %shard_map.28.held = bf16[4,640,2048]{2,1,0:T(8,128)(2,1)S(1)} custom-call(bf16[1,4,4096,640]{3,2,1,0:T(8,128)(2,1)} %a.1, bf16[1,4,4096,2048]{3,2,1,0:T(8,128)(2,1)} %g.1), custom_call_target="tpu_custom_call" | custom-call | tf_op jit(solution)/shard_map/pallas_call | solution.py:202
  178.5 4.0 %shard_map.29 = bf16[4,640,2048]{2,1,0:T(8,128)(2,1)} custom-call(bf16[4,640,2048]{2,1,0:T(8,128)(2,1)S(1)} %shard_map.28.held), custom_call_target="tpu_custom_call" | custom-call | tf_op jit(solution)/shard_map/pallas_call | solution.py:222

commit v4 on v3

v4 whole, which is shorter than its diff:
```python
import functools

import jax
import jax.numpy as jnp
from jax import lax
from jax.experimental import pallas as pl
from jax.experimental.pallas import tpu as pltpu
from jax.sharding import PartitionSpec as P

MESH = pl.DeviceIdType.MESH
RIGHT, LEFT = 0, 1
FAR, RAW, SUM, WHOLE, ON = range(5)
CUT = ON
G_SLOTS = 4
A_UNIT = 3
STRIP = 128
CUTS = (1, 1, 1, 2, 2, 3)
VMEM_LIMIT = 53000000


def kernel(n, a, g, out, abuf, gbuf, term, snd, rcv, a_sem, g_sem, c_sem, send_sem, far_sem, near_sem, whole_sem, on_sem):
    matrices, tokens, rows = a.shape[1:]
    half = g.shape[3] // n // 2
    quarter = half // 2
    per = 2 * n
    units = matrices * per
    f32 = jnp.float32
    me = lax.axis_index("dp")
    to = [lax.rem(me + 1, n), lax.rem(me + n - 1, n)]

    def columns(owner, first, width):
        return pl.ds(pl.multiple_of(owner * (2 * half) + first, width), width)

    def block(owner, b):
        return columns(owner, b * quarter, quarter)

    def load_a(m):
        return pltpu.make_async_copy(a.at[0, m], abuf.at[lax.rem(m, 2)], a_sem.at[lax.rem(m, 2)])

    def pick(j, values):
        out = values[-1]
        for i, value in reversed(list(enumerate(values[:-1]))):
            out = jnp.where(j == i, value, out)
        return out

    order = [(2, 1), (2, 0), (1, 0), (n - 1, 1), (1, 1), (n - 1, 0), (0, 0), (0, 1)]

    def load_g(u):
        m, j = u // per, lax.rem(u, per)
        owner = lax.rem(me + pick(j, [o for o, _ in order]), n)
        slot, h = lax.rem(u, G_SLOTS), pick(j, [h for _, h in order])
        return [
            pltpu.make_async_copy(
                g.at[0, m, :, block(owner, 2 * b + h)], gbuf.at[slot, :, pl.ds(b * quarter, quarter)], g_sem.at[slot]
            )
            for b in (0, 1)
        ]

    def wait_g(u):
        slot = lax.rem(u, G_SLOTS)
        pltpu.make_async_copy(g.at[0, 0, :, pl.ds(0, half)], gbuf.at[slot], g_sem.at[slot]).wait()

    def start_g(u):
        for load in load_g(u):
            load.start()

    def copy(m, kind, way, at=()):
        if kind == WHOLE:
            src = dst = out.at[m, :, columns(me, 0, 2 * half)]
        elif kind == ON:
            src = dst = out.at[m, :, columns(to[1 - way], way * half, half)]
        else:
            step = FAR if kind > CUT else kind
            src, dst = snd.at[(m, step, way, *at)], rcv.at[(m, step, way, *at)]
        if kind == WHOLE:
            sem = whole_sem.at[m, way]
        elif kind == ON:
            sem = on_sem
        else:
            sem = near_sem.at[m] if kind in (RAW, SUM) else far_sem.at[m, way]
        return remote(src, dst, sem, way)

    def remote(src, dst, sem, way):
        return pltpu.make_async_remote_copy(
            src_ref=src,
            dst_ref=dst,
            send_sem=send_sem.at[way],
            recv_sem=sem,
            device_id={"dp": to[way]},
            device_id_type=MESH,
        )

    def wait_near(m):
        both = rcv.at[m, pl.ds(RAW, 2)]
        remote(both, both, near_sem.at[m], RIGHT).wait_recv()

    def wait_on():
        where = out.at[:, :, pl.ds(0, 2 * half)]
        remote(where, where, on_sem, RIGHT).wait_recv()

    def wait_sent(way):
        where = out.at[:, :, pl.ds(0, (n - 1) * 2 * half)]
        remote(where, where, on_sem, way).wait_send()

    def add_far(m, way):
        copy(m, FAR, way).wait_recv()
        total = term[1 + way] + rcv[m, FAR, way].astype(f32)
        snd[m, SUM, way] = total.astype(snd.dtype)
        copy(m, SUM, way).start()

    def finish(m):
        wait_near(m)
        for h in (0, 1):
            total = term[3 + 2 * lax.rem(m, 2) + h] + rcv[m, RAW, h].astype(f32)
            total = total + rcv[m, SUM, 1 - h].astype(f32)
            for b in (0, 1):
                out[m, :, block(me, 2 * b + h)] = total[:, b * quarter : (b + 1) * quarter].astype(out.dtype)
        for way in (RIGHT, LEFT):
            copy(m, WHOLE, way).start()

    def pass_on(m):
        for way in (RIGHT, LEFT):
            copy(m, WHOLE, way).wait_recv()
            copy(m, ON, way).start()

    def dot(x, y):
        return lax.dot_general(x, y, (((0,), (0,)), ((), ())), preferred_element_type=f32)

    strips = rows // STRIP
    cuts, last = [], 0
    for i, count in enumerate(CUTS):
        at = pl.ds(last % strips * STRIP, count * STRIP), pl.ds(last // strips * quarter, quarter)
        last += count
        cuts.append((CUT + 1 + i, last - 1, at))
    far = lax.rem(me + 2, n)

    def strip(r):
        return pl.ds(pl.multiple_of(r * STRIP, STRIP), STRIP)

    def load_strip(r):
        return pltpu.make_async_copy(a.at[0, 0, :, strip(r)], abuf.at[0, :, strip(r)], c_sem.at[r])

    def load_far(b):
        return pltpu.make_async_copy(g.at[0, 0, :, columns(far, b * half, half)], gbuf.at[b], c_sem.at[strips + b])

    load_strip(0).start()
    load_far(0).start()

    barrier = pltpu.get_barrier_semaphore()
    for way in (RIGHT, LEFT):
        pl.semaphore_signal(barrier, inc=1, device_id={"dp": to[way]}, device_id_type=MESH)

    for r in range(1, strips):
        load_strip(r).start()
    load_far(1).start()
    start_g(2)

    @pl.loop(0, 2 * strips)
    def _(i):
        idle = i < 0
        b = jnp.where(i < strips, 0, 1)
        r = jnp.where(idle, 0, i - b * strips)

        @pl.when((i >= 0) & (b == 0))
        def _():
            load_strip(r).wait()

        @pl.when((i == 0) | (i == strips))
        def _():
            load_far(b).wait()

        @pl.when(i == 0)
        def _():
            start_g(3)

        @pl.when(i == strips)
        def _():
            start_g(4)

        value = dot(abuf[jnp.where(idle, 1, 0), :, strip(r)], gbuf[jnp.where(idle, 3, b)])
        to_column = pl.ds(pl.multiple_of(b * quarter, quarter), quarter)
        for way, side in ((RIGHT, 1), (LEFT, 0)):
            snd[0, FAR, way, strip(r), to_column] = value[:, side * quarter : (side + 1) * quarter].astype(snd.dtype)

        @pl.when(i == 0)
        def _():
            pl.semaphore_wait(barrier, 2)

        for kind, end, at in cuts:

            @pl.when(i == end)
            def _():
                for way in (RIGHT, LEFT):
                    copy(0, kind, way, at).start()

    @pl.loop(2, units)
    def unit(u):
        m, j = u // per, lax.rem(u, per)

        @pl.when((u > 2) & (u + 3 < units))
        def _():
            start_g(u + 3)

        @pl.when(u == 3)
        def _():
            start_g(5)

        @pl.when(j == 0)
        def _():
            load_a(m).wait()

        @pl.when((j == A_UNIT) & (m + 1 < matrices))
        def _():
            load_a(m + 1).start()

        wait_g(u)
        side = lax.rem(m, 2)
        slot = pick(j, [0, 0, 0, 0, 1, 2, 3 + 2 * side, 4 + 2 * side])
        term[slot] = dot(abuf[side], gbuf[lax.rem(u, G_SLOTS)])

        for way in (RIGHT, LEFT):

            @pl.when(j == way)
            def _():
                snd[m, 0, way] = term[0].astype(snd.dtype)
                copy(m, FAR, way).start()

            @pl.when(j == 2 + way)
            def _():
                snd[m, 1, way] = term[0].astype(snd.dtype)
                copy(m, RAW, way).start()

            @pl.when(j == 4 + way)
            def _():
                add_far(m, way)

        @pl.when(j == per - 1)
        def _():
            @pl.when(m >= 1)
            def _():
                finish(m - 1)

            @pl.when(m >= 2)
            def _():
                pass_on(m - 2)

    finish(matrices - 1)
    pass_on(matrices - 2)
    pass_on(matrices - 1)

    wait_on()
    for way in (RIGHT, LEFT):
        wait_sent(way)


def write(held, out, sem):
    pieces = []
    for m in range(held.shape[0]):
        for r in range(0, held.shape[1], held.shape[1] // 2):
            at = (m, pl.ds(r, held.shape[1] // 2))
            pieces.append(pltpu.make_async_copy(held.at[at], out.at[at], sem.at[len(pieces)]))
    for piece in pieces:
        piece.start()
    for piece in pieces:
        piece.wait()


def solution(mesh):
    n = mesh.shape["dp"]

    def local(a, g):
        matrices, tokens, rows = a.shape[1:]
        wide = g.shape[3]
        half = wide // n // 2
        bf16, f32 = jnp.bfloat16, jnp.float32
        held = pl.pallas_call(
            functools.partial(kernel, n),
            out_shape=pltpu.VMEM((matrices, rows, wide), bf16),
            in_specs=[pl.BlockSpec(memory_space=pl.ANY)] * 2,
            out_specs=pl.BlockSpec(memory_space=pltpu.VMEM),
            scratch_shapes=[
                pltpu.VMEM((2, tokens, rows), bf16),
                pltpu.VMEM((G_SLOTS, tokens, half), bf16),
                pltpu.VMEM((7, rows, half), f32),
                pltpu.VMEM((matrices, 3, 2, rows, half), bf16),
                pltpu.VMEM((matrices, 3, 2, rows, half), bf16),
                pltpu.SemaphoreType.DMA((2,)),
                pltpu.SemaphoreType.DMA((G_SLOTS,)),
                pltpu.SemaphoreType.DMA((rows // STRIP + 2,)),
                pltpu.SemaphoreType.DMA((2,)),
                pltpu.SemaphoreType.DMA((matrices, 2)),
                pltpu.SemaphoreType.DMA((matrices,)),
                pltpu.SemaphoreType.DMA((matrices, 2)),
                pltpu.SemaphoreType.DMA,
            ],
            compiler_params=pltpu.CompilerParams(
                collective_id=0, has_side_effects=True, vmem_limit_bytes=VMEM_LIMIT
            ),
        )(a, g)
        return pl.pallas_call(
            write,
            out_shape=jax.ShapeDtypeStruct(held.shape, bf16),
            in_specs=[pl.BlockSpec(memory_space=pltpu.VMEM)],
            out_specs=pl.BlockSpec(memory_space=pl.ANY),
            scratch_shapes=[pltpu.SemaphoreType.DMA((2 * matrices,))],
            compiler_params=pltpu.CompilerParams(vmem_limit_bytes=2 * 1024 * 1024),
        )(pltpu.with_memory_space_constraint(held, pltpu.VMEM))

    return jax.shard_map(
        local,
        mesh=mesh,
        in_specs=(P(("rep", "dp")), P(("rep", "dp"))),
        out_specs=P("rep"),
        check_vma=False,
    )
```

time: 183 us -> 180 us (0.984)
  Pallas kernels: 183 us -> 180 us
    pallas_call x1, Pallas kernels: 178 us -> 176 us  [local(): pl.pallas_call(functools.partial(kernel, n), out_shape=pltpu.VMEM((matric...]
where the time goes in v4:
time: 180 us
  Pallas kernels  180 us (100%)
    pallas_call x1, Pallas kernels, local(): pl.pallas_call(functools.partial(kernel, n), out_shape=pltpu.VMEM((matric...  176 us
    pallas_call x1, Pallas kernels, local(): pl.pallas_call(write, out_shape=jax.ShapeDtypeStruct(held.shape, bf16), i...  4.04 us

profile of v4, /device:TPU:112, one launch (start us, length us, event | category | flops | bytes accessed | tf_op | source)
XLA Modules:
  0.0 180.3 jit_solution(9280700863640244238)
XLA Ops:
  0.0 176.3 %shard_map.28.held = bf16[4,640,2048]{2,1,0:T(8,128)(2,1)S(1)} custom-call(bf16[1,4,4096,640]{3,2,1,0:T(8,128)(2,1)} %a.1, bf16[1,4,4096,2048]{3,2,1,0:T(8,128)(2,1)} %g.1), custom_call_target="tpu_custom_call" | custom-call | tf_op jit(solution)/shard_map/pallas_call | solution.py:276
  176.3 4.0 %shard_map.29 = bf16[4,640,2048]{2,1,0:T(8,128)(2,1)} custom-call(bf16[4,640,2048]{2,1,0:T(8,128)(2,1)S(1)} %shard_map.28.held), custom_call_target="tpu_custom_call" | custom-call | tf_op jit(solution)/shard_map/pallas_call | solution.py:300

commit v5 on v4

--- a/solution.py
+++ b/solution.py
@@ -10,9 +10,9 @@
 MESH = pl.DeviceIdType.MESH
 RIGHT, LEFT = 0, 1
 FAR, RAW, SUM, WHOLE, ON = range(5)
-CUT = ON
 G_SLOTS = 4
 A_UNIT = 3
+CHUNKS = 2
 STRIP = 128
 CUTS = (1, 1, 1, 2, 2, 3)
 VMEM_LIMIT = 53000000
@@ -70,8 +70,7 @@
         elif kind == ON:
             src = dst = out.at[m, :, columns(to[1 - way], way * half, half)]
         else:
-            step = FAR if kind > CUT else kind
-            src, dst = snd.at[(m, step, way, *at)], rcv.at[(m, step, way, *at)]
+            src, dst = snd.at[(m, kind, way, *at)], rcv.at[(m, kind, way, *at)]
         if kind == WHOLE:
             sem = whole_sem.at[m, way]
         elif kind == ON:
@@ -128,23 +127,33 @@
 
     strips = rows // STRIP
     cuts, last = [], 0
-    for i, count in enumerate(CUTS):
+    for count in CUTS:
         at = pl.ds(last % strips * STRIP, count * STRIP), pl.ds(last // strips * quarter, quarter)
         last += count
-        cuts.append((CUT + 1 + i, last - 1, at))
+        cuts.append((last - 1, at))
     far = lax.rem(me + 2, n)
 
     def strip(r):
         return pl.ds(pl.multiple_of(r * STRIP, STRIP), STRIP)
 
     def load_strip(r):
-        return pltpu.make_async_copy(a.at[0, 0, :, strip(r)], abuf.at[0, :, strip(r)], c_sem.at[r])
+        return pltpu.make_async_copy(a.at[0, 0, :, strip(r)], abuf.at[0, :, strip(r)], c_sem.at[2 * CHUNKS - 1 + r])
 
     def load_far(b):
-        return pltpu.make_async_copy(g.at[0, 0, :, columns(far, b * half, half)], gbuf.at[b], c_sem.at[strips + b])
-
-    load_strip(0).start()
-    load_far(0).start()
+        return pltpu.make_async_copy(g.at[0, 0, :, columns(far, b * half, half)], gbuf.at[b], g_sem.at[b])
+
+    chunks = [pl.ds(c * (tokens // CHUNKS), tokens // CHUNKS) for c in range(CHUNKS)]
+
+    def load_first(c):
+        at, cut = chunks[c], pl.ds(0, STRIP)
+        return [
+            pltpu.make_async_copy(a.at[0, 0, at, cut], abuf.at[0, at, cut], c_sem.at[c]),
+            pltpu.make_async_copy(g.at[0, 0, at, columns(far, 0, half)], gbuf.at[0, at], c_sem.at[CHUNKS + c]),
+        ]
+
+    for c in range(CHUNKS):
+        for load in load_first(c):
+            load.start()
 
     barrier = pltpu.get_barrier_semaphore()
     for way in (RIGHT, LEFT):
@@ -155,43 +164,48 @@
     load_far(1).start()
     start_g(2)
 
-    @pl.loop(0, 2 * strips)
-    def _(i):
-        idle = i < 0
-        b = jnp.where(i < strips, 0, 1)
-        r = jnp.where(idle, 0, i - b * strips)
-
-        @pl.when((i >= 0) & (b == 0))
-        def _():
-            load_strip(r).wait()
-
-        @pl.when((i == 0) | (i == strips))
-        def _():
-            load_far(b).wait()
-
-        @pl.when(i == 0)
-        def _():
-            start_g(3)
-
-        @pl.when(i == strips)
-        def _():
-            start_g(4)
-
-        value = dot(abuf[jnp.where(idle, 1, 0), :, strip(r)], gbuf[jnp.where(idle, 3, b)])
+    def keep_far(b, r, value):
         to_column = pl.ds(pl.multiple_of(b * quarter, quarter), quarter)
         for way, side in ((RIGHT, 1), (LEFT, 0)):
-            snd[0, FAR, way, strip(r), to_column] = value[:, side * quarter : (side + 1) * quarter].astype(snd.dtype)
-
-        @pl.when(i == 0)
-        def _():
-            pl.semaphore_wait(barrier, 2)
-
-        for kind, end, at in cuts:
+            piece = value[:, side * quarter : (side + 1) * quarter]
+            snd[0, FAR, way, strip(r), to_column] = piece.astype(snd.dtype)
+
+    def send_far(at):
+        for way in (RIGHT, LEFT):
+            copy(0, FAR, way, at).start()
+
+    value = None
+    for c in range(CHUNKS):
+        for load in load_first(c):
+            load.wait()
+        product = dot(abuf[0, chunks[c], pl.ds(0, STRIP)], gbuf[0, chunks[c]])
+        value = product if value is None else value + product
+    keep_far(0, 0, value)
+    pl.semaphore_wait(barrier, 2)
+    send_far(cuts[0][1])
+    start_g(3)
+
+    @pl.loop(1, 2 * strips)
+    def _(i):
+        b = i // strips
+        r = lax.rem(i, strips)
+
+        @pl.when(b == 0)
+        def _():
+            load_strip(r).wait()
+
+        @pl.when(i == strips)
+        def _():
+            load_far(1).wait()
+            start_g(4)
+
+        keep_far(b, r, dot(abuf[0, :, strip(r)], gbuf[b]))
+
+        for end, at in cuts[1:]:
 
             @pl.when(i == end)
             def _():
-                for way in (RIGHT, LEFT):
-                    copy(0, kind, way, at).start()
+                send_far(at)
 
     @pl.loop(2, units)
     def unit(u):
@@ -254,15 +268,12 @@
 
 
 def write(held, out, sem):
-    pieces = []
+    pieces = [held.shape[1] // 2 * i for i in (0, 1)]
     for m in range(held.shape[0]):
-        for r in range(0, held.shape[1], held.shape[1] // 2):
+        for r in pieces:
             at = (m, pl.ds(r, held.shape[1] // 2))
-            pieces.append(pltpu.make_async_copy(held.at[at], out.at[at], sem.at[len(pieces)]))
-    for piece in pieces:
-        piece.start()
-    for piece in pieces:
-        piece.wait()
+            pltpu.make_async_copy(held.at[at], out.at[at], sem).start()
+    pltpu.make_async_copy(held, out, sem).wait()
 
 
 def solution(mesh):
@@ -286,7 +297,7 @@
                 pltpu.VMEM((matrices, 3, 2, rows, half), bf16),
                 pltpu.SemaphoreType.DMA((2,)),
                 pltpu.SemaphoreType.DMA((G_SLOTS,)),
-                pltpu.SemaphoreType.DMA((rows // STRIP + 2,)),
+                pltpu.SemaphoreType.DMA((2 * CHUNKS + rows // STRIP - 1,)),
                 pltpu.SemaphoreType.DMA((2,)),
                 pltpu.SemaphoreType.DMA((matrices, 2)),
                 pltpu.SemaphoreType.DMA((matrices,)),
@@ -302,7 +313,7 @@
             out_shape=jax.ShapeDtypeStruct(held.shape, bf16),
             in_specs=[pl.BlockSpec(memory_space=pltpu.VMEM)],
             out_specs=pl.BlockSpec(memory_space=pl.ANY),
-            scratch_shapes=[pltpu.SemaphoreType.DMA((2 * matrices,))],
+            scratch_shapes=[pltpu.SemaphoreType.DMA],
             compiler_params=pltpu.CompilerParams(vmem_limit_bytes=2 * 1024 * 1024),
         )(pltpu.with_memory_space_constraint(held, pltpu.VMEM))
 

time: 180 us -> 180 us (level)
  no operation moved by 1% of the time
where the time goes in v5:
time: 180 us
  Pallas kernels  180 us (100%)
    pallas_call x1, Pallas kernels, local(): pl.pallas_call(functools.partial(kernel, n), out_shape=pltpu.VMEM((matric...  176 us
    pallas_call x1, Pallas kernels, local(): pl.pallas_call(write, out_shape=jax.ShapeDtypeStruct(held.shape, bf16), i...  3.97 us

profile of v5, /device:TPU:112, one launch (start us, length us, event | category | flops | bytes accessed | tf_op | source)
XLA Modules:
  0.0 180.2 jit_solution(11979088349937781036)
XLA Ops:
  0.0 176.2 %shard_map.28.held = bf16[4,640,2048]{2,1,0:T(8,128)(2,1)S(1)} custom-call(bf16[1,4,4096,640]{3,2,1,0:T(8,128)(2,1)} %a.1, bf16[1,4,4096,2048]{3,2,1,0:T(8,128)(2,1)} %g.1), custom_call_target="tpu_custom_call" | custom-call | tf_op jit(solution)/shard_map/pallas_call | solution.py:287
  176.2 4.0 %shard_map.29 = bf16[4,640,2048]{2,1,0:T(8,128)(2,1)} custom-call(bf16[4,640,2048]{2,1,0:T(8,128)(2,1)S(1)} %shard_map.28.held), custom_call_target="tpu_custom_call" | custom-call | tf_op jit(solution)/shard_map/pallas_call | solution.py:311

commit v6 on v5

--- a/solution.py
+++ b/solution.py
@@ -14,7 +14,7 @@
 A_UNIT = 3
 CHUNKS = 2
 STRIP = 128
-CUTS = (1, 1, 1, 2, 2, 3)
+CUTS = (1, 1, 1, 1, 1, 1, 2, 2)
 VMEM_LIMIT = 53000000
 
 

time: 180 us -> 180 us (level)
  no operation moved by 1% of the time
where the time goes in v6:
time: 180 us
  Pallas kernels  180 us (100%)
    pallas_call x1, Pallas kernels, local(): pl.pallas_call(functools.partial(kernel, n), out_shape=pltpu.VMEM((matric...  176 us
    pallas_call x1, Pallas kernels, local(): pl.pallas_call(write, out_shape=jax.ShapeDtypeStruct(held.shape, bf16), i...  3.97 us

profile of v6, /device:TPU:112, one launch (start us, length us, event | category | flops | bytes accessed | tf_op | source)
XLA Modules:
  0.0 180.1 jit_solution(7456090754193808648)
XLA Ops:
  0.0 176.1 %shard_map.28.held = bf16[4,640,2048]{2,1,0:T(8,128)(2,1)S(1)} custom-call(bf16[1,4,4096,640]{3,2,1,0:T(8,128)(2,1)} %a.1, bf16[1,4,4096,2048]{3,2,1,0:T(8,128)(2,1)} %g.1), custom_call_target="tpu_custom_call" | custom-call | tf_op jit(solution)/shard_map/pallas_call | solution.py:287
  176.2 4.0 %shard_map.29 = bf16[4,640,2048]{2,1,0:T(8,128)(2,1)} custom-call(bf16[4,640,2048]{2,1,0:T(8,128)(2,1)S(1)} %shard_map.28.held), custom_call_target="tpu_custom_call" | custom-call | tf_op jit(solution)/shard_map/pallas_call | solution.py:311
